TPU v7x, 256 devices: a whole 4x4x8 slice. The times are simulated.
256 devices in a mesh: seq: 16 (over z, core), tp: 16 (over y, x).
Axes of the slice: x: 4, y: 4, z: 8, core: 2. Of those that a mesh axis runs over, the one named last changes fastest.
Arguments:
- tokens: bfloat16 [4096, 4608], P('seq', 'tp'), may hold values from -6 to 6
- attention_gain: float32 [4608], replicated, may hold values from 0.25 to 1.75
- query_weight: bfloat16 [4608, 4096], P(None, 'tp'), may hold values from -0.09375 to 0.09375
- key_weight: bfloat16 [4608, 2048], P(None, 'tp'), may hold values from -0.09375 to 0.09375
- value_weight: bfloat16 [4608, 2048], P(None, 'tp'), may hold values from -0.09375 to 0.09375
- output_weight: bfloat16 [4096, 4608], P('tp'), may hold values from -0.09375 to 0.09375
- post_gain: float32 [4608], replicated, may hold values from 0.25 to 1.75
- local_gain: float32 [4608], replicated, may hold values from 0.25 to 1.75
- local_query_weight: bfloat16 [4608, 4096], P(None, 'tp'), may hold values from -0.09375 to 0.09375
- local_key_weight: bfloat16 [4608, 2048], P(None, 'tp'), may hold values from -0.09375 to 0.09375
- local_value_weight: bfloat16 [4608, 2048], P(None, 'tp'), may hold values from -0.09375 to 0.09375
Outputs:
- hidden: bfloat16 [4096, 4608], P('seq', 'tp')
- local_heads: bfloat16 [4096, 4096], P('seq', 'tp')
All inputs are finite; a program needn't handle non-finite values.
Results may differ from a plain program's by a relative error of at most 0.02.
Values may be sent and summed in bfloat16 or wider, within the bound.
A program may use at most 128 MiB of HBM per device.

v0:
```python
import jax
import jax.numpy as jnp
from jax import lax
from jax.sharding import PartitionSpec as P

D = 4608
HEADS = 32
HEAD_DIM = 128


SOFT_CAP = 50.0
NORM_EPS = 1e-06


def side_by_side(arrays, axis, dim, along):
    widths = [a.shape[along] for a in arrays]
    both = jnp.concatenate(arrays, axis=along)
    result = lax.all_gather(both, axis, axis=dim, tiled=True)
    return tuple(jnp.split(result, [sum(widths[:k]) for k in range(1, len(widths))], axis=along))


def joined_along(blocks, dim):
    dims = list(blocks.shape[1:])
    dims[dim] *= blocks.shape[0]
    return jnp.moveaxis(blocks, 0, dim).reshape(dims)


def copy_for_each(array, axis):
    devices = lax.axis_size(axis)
    return lax.all_to_all(
        jnp.broadcast_to(array[None], (devices, *array.shape)), axis, 0, 0, tiled=True
    )


def gather_directly(array, axis, dim):
    return joined_along(copy_for_each(array, axis), dim)


def split_up(array, dim, devices):
    before, after = (array.shape[:dim], array.shape[dim + 1 :])
    return jnp.moveaxis(array.reshape(*before, devices, -1, *after), dim, 0)


def sent_and_summed(array, axis, dim):
    blocks = split_up(array, dim, lax.axis_size(axis))
    arrived = lax.all_to_all(blocks, axis, split_axis=0, concat_axis=0, tiled=True)
    return arrived.astype(jnp.float32).sum(axis=0)


def passed_along(value, axis, steps):
    count = lax.axis_size(axis)
    leading, last = (max(0, -steps), min(count, count - steps))
    return lax.ppermute(value, axis, [(source, source + steps) for source in range(leading, last)])


def rms_scaled(values, weights):
    widened = values.astype(jnp.float32)
    factor = lax.rsqrt(jnp.mean(widened * widened, axis=-1, keepdims=True) + NORM_EPS)
    return widened * factor * weights


def rotate(vectors, places):
    head_size = vectors.shape[-1]
    halfway = head_size // 2
    exponents = jnp.arange(halfway, dtype=jnp.float32) * (2.0 / head_size)
    frequency = jnp.power(jnp.float32(10000.0), -exponents)
    angles = places.astype(jnp.float32)[:, None] * frequency[None, :]
    cosine_part = jnp.cos(angles)[:, None, :]
    sine_part = jnp.sin(angles)[:, None, :]
    first_half = vectors[..., :halfway]
    second_half = vectors[..., halfway:]
    return jnp.concatenate(
        [
            first_half * cosine_part - second_half * sine_part,
            second_half * cosine_part + first_half * sine_part,
        ],
        axis=-1,
    )


def project_heads(normed, weight_query, weight_key, weight_value, places):
    row_count = normed.shape[0]
    queries = jnp.dot(normed, weight_query, preferred_element_type=jnp.float32).reshape(
        row_count, -1, HEAD_DIM
    )
    key_heads = jnp.dot(normed, weight_key, preferred_element_type=jnp.float32).reshape(
        row_count, -1, HEAD_DIM
    )
    value_heads = jnp.dot(normed, weight_value, preferred_element_type=jnp.float32).reshape(
        row_count, -1, HEAD_DIM
    )
    return (
        rotate(queries, places).astype(jnp.bfloat16),
        rotate(key_heads, places).astype(jnp.bfloat16),
        value_heads.astype(jnp.bfloat16),
    )


def empty_carry(queries, kv_heads):
    row_count = queries.shape[0]
    groups = queries.shape[1] // kv_heads
    return (
        jnp.zeros((row_count, kv_heads, groups, HEAD_DIM), jnp.float32),
        jnp.zeros((kv_heads, groups, row_count), jnp.float32),
    )


def attend_block(queries, query_places, key_block, value_block, key_places, window_size):
    kv_heads = key_block.shape[1]
    groups = queries.shape[1] // kv_heads
    grouped = queries.reshape(queries.shape[0], kv_heads, groups, queries.shape[2])
    scale = float(D // HEADS) ** (-0.5)
    scores = (
        jnp.einsum("qhrd,khd->hrqk", grouped, key_block, preferred_element_type=jnp.float32) * scale
    )
    scores = SOFT_CAP * jnp.tanh(scores / SOFT_CAP)
    offset = query_places[:, None] - key_places[None, :]
    allowed = (offset >= 0) & (key_places >= 0)[None, :]
    if window_size is not None:
        allowed = allowed & (offset < window_size)
    weights = jnp.where(allowed[None, None], jnp.exp(scores), jnp.float32(0.0))
    denominator = jnp.sum(weights, axis=-1)
    numerator = jnp.einsum(
        "hrqk,khd->qhrd",
        weights.astype(jnp.bfloat16),
        value_block,
        preferred_element_type=jnp.float32,
    )
    return (numerator, denominator)


def finish_heads(running):
    numerator, denominator = running
    averaged = numerator / jnp.transpose(denominator, (2, 0, 1))[..., None]
    return averaged.astype(jnp.bfloat16).reshape(numerator.shape[0], -1)


def visit_one(partial_sum, query_set, key_block, value_block, key_places, needed):

    def compute(current):
        return attend_block(query_set[0], query_set[1], key_block, value_block, key_places, None)

    return lax.cond(needed, compute, lambda current: current, partial_sum)


def causal_sets(query_sets, key_heads, value_heads):
    kv_heads = key_heads.shape[1]
    initial = tuple((empty_carry(query_set[0], kv_heads) for query_set in query_sets))
    latest = tuple((jnp.max(query_set[1]) for query_set in query_sets))
    first_row = jnp.int32(0)
    key_block, value_block = side_by_side((key_heads, value_heads), "seq", 0, 1)
    key_places = lax.iota(jnp.int32, key_block.shape[0])
    updated = []
    for query_set, visit_partial_sum, newest in zip(query_sets, initial, latest):
        updated.append(
            visit_one(
                visit_partial_sum,
                query_set,
                key_block,
                value_block,
                key_places,
                first_row <= newest,
            )
        )
    totals = tuple(updated)
    return [finish_heads(partial_sum) for partial_sum in totals]


def local(
    tokens,
    attention_gain,
    query_weight,
    key_weight,
    value_weight,
    output_weight,
    post_gain,
    local_gain,
    local_query_weight,
    local_key_weight,
    local_value_weight,
):
    row_count = tokens.shape[0]
    column_count = tokens.shape[1]
    section_index = lax.axis_index("seq")
    places = section_index * row_count + lax.iota(jnp.int32, row_count)
    full_rows = gather_directly(tokens, "tp", 1)
    normed = rms_scaled(full_rows, attention_gain).astype(jnp.bfloat16)
    queries, key_heads, value_heads = project_heads(
        normed, query_weight, key_weight, value_weight, places
    )
    attended = causal_sets([(queries, places)], key_heads, value_heads)[0]
    share_rows = row_count // lax.axis_size("tp")
    summed = sent_and_summed(
        jnp.dot(attended, output_weight, preferred_element_type=jnp.float32).astype(jnp.bfloat16),
        "tp",
        0,
    )
    own_tokens = lax.dynamic_slice_in_dim(
        full_rows, lax.axis_index("tp") * share_rows, share_rows, 0
    )
    hidden_share = (own_tokens.astype(jnp.float32) + rms_scaled(summed, post_gain)).astype(
        jnp.bfloat16
    )
    whole_hidden = gather_directly(hidden_share, "tp", 0)
    hidden = lax.dynamic_slice_in_dim(
        whole_hidden, lax.axis_index("tp") * column_count, column_count, 1
    )
    local_normed = rms_scaled(whole_hidden, local_gain).astype(jnp.bfloat16)
    local_queries, local_keys, local_values = project_heads(
        local_normed, local_query_weight, local_key_weight, local_value_weight, places
    )
    window_size = row_count // 2
    tails = jnp.stack(
        [local_keys[row_count - window_size :], local_values[row_count - window_size :]]
    )
    earlier = passed_along(tails, "seq", 1)
    key_block = jnp.concatenate([earlier[0], local_keys], axis=0)
    value_block = jnp.concatenate([earlier[1], local_values], axis=0)
    key_places = (
        section_index * row_count - window_size + lax.iota(jnp.int32, window_size + row_count)
    )
    result = attend_block(local_queries, places, key_block, value_block, key_places, window_size)
    local_heads = finish_heads(result)
    return (hidden, local_heads)


def solution(mesh):
    in_specs = (
        P("seq", "tp"),
        P(),
        P(None, "tp"),
        P(None, "tp"),
        P(None, "tp"),
        P("tp", None),
        P(),
        P(),
        P(None, "tp"),
        P(None, "tp"),
        P(None, "tp"),
    )
    out_specs = (P("seq", "tp"), P("seq", "tp"))
    return jax.shard_map(local, mesh=mesh, in_specs=in_specs, out_specs=out_specs, check_vma=False)
```

profile of v0, /device:TPU:1, one launch (start us, length us, event | category | flops | bytes accessed | tf_op | source)
XLA Modules:
  0.0 234.4 jit_solution(2536734655906599384)
XLA Ops:
  7.2 0.0 copy-start
  7.2 2.7 %broadcast_in_dim.34 = bf16[16,256,288]{1,2,0:T(8,128)(2,1)} broadcast(bf16[256,288]{0,1:T(8,128)(2,1)} %param.13), dimensions={1,2} | broadcast | bytes 2506752 | tf_op jit(solution)/shard_map/broadcast_in_dim | solution.py:31
  9.9 7.6 %all-to-all-start = ((bf16[16,256,288]{1,2,0:T(8,128)(2,1)}), bf16[16,256,288]{1,2,0:T(8,128)(2,1)}, u32[]{:S(2)}, u32[]{:S(2)}) async-start(bf16[16,256,288]{1,2,0:T(8,128)(2,1)} %broadcast_in_dim.34), calls=%async_computation | async-start | bytes 4718592 | tf_op jit(solution)/shard_map/all_to_all | solution.py:30
  17.5 0.0 copy-start.10
  17.5 0.0 all-gather.2.cloned.1.call-start
  17.6 0.0 copy-start.14
  17.6 0.0 copy-start.12
  17.6 34.8 %all-to-all-done = bf16[16,256,288]{1,2,0:T(8,128)(2,1)} async-done(((bf16[16,256,288]{1,2,0:T(8,128)(2,1)}), bf16[16,256,288]{1,2,0:T(8,128)(2,1)}, u32[]{:S(2)}, u32[]{:S(2)}) %all-to-all-start) | async-done | bytes 2359328 | tf_op jit(solution)/shard_map/all_to_all | solution.py:30
  52.5 2.4 %fusion.7 = f32[256]{0:T(256)S(1)} fusion(bf16[16,256,288]{1,2,0:T(8,128)(2,1)} %all-to-all-done), kind=kLoop, calls=%fused_computation.15 | loop fusion | flops 3538688 | bytes 2360320 | tf_op jit(solution)/shard_map/reduce_sum | solution.py:58
  54.9 0.0 copy-start.18
  54.9 3.9 %fusion.18 = bf16[256,1,128]{0,2,1:T(8,128)(2,1)S(1)} fusion(bf16[4608,128]{1,0:T(8,128)(2,1)S(1)} %copy-done.17, bf16[256,4608]{0,1:T(8,128)(2,1)} %bitcast.12, f32[4608]{0:T(1024)S(1)} %copy-done.10, f32[256]{0:T(256)S(1)} %add_rsqrt_fusion.1), kind=kOutput, calls=%fused_computation.35 | convolution fusion | flops 306741248 | bytes 3623936 | tf_op jit(solution)/shard_map/dot_general | solution.py:89
  58.8 3.8 %convolution_bitcast_fusion.2 = f32[256,1,128]{0,2,1:T(8,128)S(1)} fusion(bf16[4608,128]{1,0:T(8,128)(2,1)S(1)} %copy-done.18, bf16[256,4608]{0,1:T(8,128)(2,1)} %bitcast.12, f32[4608]{0:T(1024)S(1)} %copy-done.10, f32[256]{0:T(256)S(1)} %add_rsqrt_fusion.1), kind=kOutput, calls=%fused_computation.32 | convolution fusion | flops 306708480 | bytes 3689472 | tf_op jit(solution)/shard_map/dot_general | solution.py:86
  62.6 0.3 fusion.43
  62.9 0.7 pad_maximum_fusion
  63.6 0.0 all-gather.2.cloned.1.call-update
  63.6 0.6 fusion.52
  64.2 0.1 mul.266
  65.0 4.4 %copy.66 = bf16[256,4608]{1,0:T(8,128)(2,1)} copy(bf16[256,4608]{0,1:T(8,128)(2,1)} %bitcast.108) | data formatting | bytes 4718592 | tf_op jit(solution)/shard_map/dot_general | solution.py:83
  69.3 0.6 iota_add_fusion.1
  69.9 0.3 multiply_cosine_fusion
  70.3 2.2 fusion.9
  72.5 0.2 copy-done.2
  72.7 0.8 fusion.57
  73.5 31.8 %all-gather.2.cloned.1.call-done = bf16[4096,2,128]{0,2,1:T(8,128)(2,1)} async-done(((bf16[256,2,128]{0,2,1:T(8,128)(2,1)}), bf16[4096,2,128]{0,2,1:T(8,128)(2,1)}) %all-gather.2.cloned.1.call-update) | async-done | bytes 2097168 | tf_op jit(solution)/shard_map/all_gather | solution.py:18
  105.4 13.2 %conditional.1 = (f32[1,2,256]{2,1,0:T(2,128)}, f32[256,1,2,128]{0,3,2,1:T(8,128)}) conditional(s32[]{:T(128)} %convert_element_type.102, () %tuple.16, (s32[256]{0:T(256)}, s32[4096]{0:T(1024)S(1)}, s32[4096]{0:T(1024)S(1)}, bf16[4096,2,128]{0,2,1:T(8,128)(2,1)}, bf16[256,2,128]{0,2,1:T(8,128)(2,1)S(1)}) %tuple.17), branch_computations={%region_2.0_spmd, %region_3.5_spmd} | conditional | flops 1087376896 | bytes 26127404 | solution.py:143
  105.4 2.1 fusion.3
  107.5 4.1 %copy.47 = bf16[4096,2,128]{2,0,1:T(8,128)(2,1)} copy(bf16[4096,2,128]{0,2,1:T(8,128)(2,1)} %get-tuple-element.40) | data formatting | bytes 4194304 | tf_op jit(solution)/shard_map
  111.6 4.9 %fusion.55 = (f32[2,256]{1,0:T(2,128)}, bf16[1,2,256,4096]{2,3,1,0:T(8,128)(2,1)S(1)}) fusion(bf16[256,2,128]{0,2,1:T(8,128)(2,1)S(1)} %get-tuple-element.41, bf16[4096,2,128]{2,0,1:T(8,128)(2,1)} %copy.47, pred[256,4096]{0,1:T(8,128)(4,1)S(1)} %fusion.3), kind=kOutput, calls=%fused_computation.103 | convolution fusion | flops 547356160 | bytes 6424576 | tf_op jit(solution)/shard_map/cond/branch_1_fun/qhrd,khd->hrqk/dot_general | solution.py:114
  116.4 1.3 fusion.4
  117.7 0.8 copy.70
  118.6 1.0 divide_convert_fusion
  119.5 0.0 copy-done
  119.5 2.2 convolution_convert_fusion
  121.8 6.6 %all-to-all-start.1 = ((bf16[16,16,4608]{2,1,0:T(8,128)(2,1)}), bf16[16,16,4608]{2,1,0:T(8,128)(2,1)}, u32[]{:S(2)}, u32[]{:S(2)}) async-start(bf16[16,16,4608]{2,1,0:T(8,128)(2,1)} %bitcast.107), calls=%async_computation.1 | async-start | bytes 4718592 | tf_op jit(solution)/shard_map/all_to_all | solution.py:46
  128.4 1.7 constant_dynamic-slice_fusion.1
  130.0 1.0 copy.71
  131.1 33.7 %all-to-all-done.1 = bf16[16,16,4608]{2,1,0:T(8,128)(2,1)} async-done(((bf16[16,16,4608]{2,1,0:T(8,128)(2,1)}), bf16[16,16,4608]{2,1,0:T(8,128)(2,1)}, u32[]{:S(2)}, u32[]{:S(2)}) %all-to-all-start.1) | async-done | bytes 2359328 | tf_op jit(solution)/shard_map/all_to_all | solution.py:46
  164.7 2.0 convert_reduce_fusion
  166.7 0.2 multiply_reduce_fusion
  166.9 0.0 copy-done.4
  166.9 0.1 add_convert_fusion
  167.0 1.7 broadcast_in_dim.35
  168.7 4.6 %all-to-all-start.2 = ((bf16[16,16,4608]{2,1,0:T(8,128)(2,1)}), bf16[16,16,4608]{2,1,0:T(8,128)(2,1)}, u32[]{:S(2)}, u32[]{:S(2)}) async-start(bf16[16,16,4608]{2,1,0:T(8,128)(2,1)} %broadcast_in_dim.35), calls=%async_computation.2 | async-start | bytes 4718592 | tf_op jit(solution)/shard_map/all_to_all | solution.py:30
  173.3 4.4 %copy.68 = bf16[256,4608]{1,0:T(8,128)(2,1)} copy(bf16[256,4608]{0,1:T(8,128)(2,1)} %bitcast.109) | data formatting | bytes 4718592 | tf_op jit(solution)/shard_map/dot_general | solution.py:83
  177.7 0.2 fusion.24
  177.9 28.8 %all-to-all-done.2 = bf16[16,16,4608]{2,1,0:T(8,128)(2,1)} async-done(((bf16[16,16,4608]{2,1,0:T(8,128)(2,1)}), bf16[16,16,4608]{2,1,0:T(8,128)(2,1)}, u32[]{:S(2)}, u32[]{:S(2)}) %all-to-all-start.2) | async-done | bytes 2359328 | tf_op jit(solution)/shard_map/all_to_all | solution.py:30
  206.7 2.2 fusion.10
  208.9 0.1 rsqrt.31
  209.1 0.0 copy-start.19
  209.1 3.1 %convolution_convert_fusion.1 = bf16[256,128]{0,1:T(8,128)(2,1)S(1)} fusion(bf16[4608,128]{1,0:T(8,128)(2,1)} %param.23, bf16[256,4608]{1,0:T(8,128)(2,1)} %bitcast.24, f32[4608]{0:T(1024)S(1)} %copy-done.11, f32[256]{0:T(256)S(1)} %rsqrt.31), kind=kOutput, calls=%fused_computation.33 | convolution fusion | flops 306741248 | bytes 3623936 | tf_op jit(solution)/shard_map/dot_general | solution.py:89
  212.2 2.7 %convolution_bitcast_fusion.1 = f32[256,1,128]{0,2,1:T(8,128)S(1)} fusion(bf16[4608,128]{1,0:T(8,128)(2,1)S(1)} %copy-done.19, bf16[256,4608]{1,0:T(8,128)(2,1)} %bitcast.24, f32[4608]{0:T(1024)S(1)} %copy-done.11, f32[256]{0:T(256)S(1)} %rsqrt.31), kind=kOutput, calls=%fused_computation.31 | convolution fusion | flops 306708480 | bytes 3689472 | tf_op jit(solution)/shard_map/dot_general | solution.py:86
  215.0 0.3 fusion.47
  215.4 0.0 copy-start.1
  215.4 5.6 %collective-permute-start = (bf16[2,128,1,128]{1,3,2,0:T(8,128)(2,1)S(1)}, bf16[2,128,1,128]{1,3,2,0:T(8,128)(2,1)S(1)}, u32[]{:S(2)}, u32[]{:S(2)}) collective-permute-start(bf16[2,128,1,128]{1,3,2,0:T(8,128)(2,1)S(1)} %pad_maximum_fusion.2), channel_id=1, source_target_pairs={{0,16},{16,32},{32,48},{48,64},{64,80},{80,96},{96,112},{112,128},... | collective-permute-start | bytes 196616 | tf_op jit(solution)/shard_map/ppermute | solution.py:53
  221.0 2.3 fusion.12
  223.3 0.8 fusion.58
  224.1 0.0 copy-done.6
  224.2 0.0 copy-done.8
  224.2 1.1 constant_dynamic-slice_fusion
  225.3 0.8 copy.55
  226.1 0.0 collective-permute-done
  226.1 0.4 fusion.56
  226.5 0.2 fusion.20
  226.8 0.8 copy.56
  (44 shorter events, 0.2 us)
Async XLA Ops:
  7.2 112.4 %copy-start = (bf16[256,4608]{1,0:T(8,128)(2,1)S(1)}, bf16[256,4608]{1,0:T(8,128)(2,1)}, u32[]{:S(2)}) copy-start(bf16[256,4608]{1,0:T(8,128)(2,1)} %param.18) | copy-start | bytes 7077892
  9.9 42.6 %all-to-all-start = ((bf16[16,256,288]{1,2,0:T(8,128)(2,1)}), bf16[16,256,288]{1,2,0:T(8,128)(2,1)}, u32[]{:S(2)}, u32[]{:S(2)}) async-start(bf16[16,256,288]{1,2,0:T(8,128)(2,1)} %broadcast_in_dim.34), calls=%async_computation | async-start | bytes 4718592 | tf_op jit(solution)/shard_map/all_to_all | solution.py:30
  17.5 37.4 %copy-start.10 = (f32[4608]{0:T(1024)S(1)}, f32[4608]{0:T(1024)}, u32[]{:S(2)}) copy-start(f32[4608]{0:T(1024)} %param.14) | copy-start | bytes 55300
  17.5 87.9 %all-gather.2.cloned.1.call-start = ((), (), s32[]{:S(2)}) async-start(), calls=%async_computation.3 | async-start | bytes 2228224 | tf_op jit(solution)/shard_map/all_gather | solution.py:18
  17.6 52.3 %copy-start.14 = (f32[64]{0:T(128)}, f32[64]{0:T(128)S(1)}, u32[]{:S(2)}) copy-start(f32[64]{0:T(128)S(1)} %negate_power_fusion) | copy-start | bytes 772
  17.6 52.3 %copy-start.12 = (f32[256]{0:T(256)}, f32[256]{0:T(256)S(1)}, u32[]{:S(2)}) copy-start(f32[256]{0:T(256)S(1)} %fusion.51) | copy-start | bytes 3076
  52.5 2.4 %copy-start.17 = (bf16[4608,128]{1,0:T(8,128)(2,1)S(1)}, bf16[4608,128]{1,0:T(8,128)(2,1)}, u32[]{:S(2)}) copy-start(bf16[4608,128]{1,0:T(8,128)(2,1)} %param.17) | copy-start | bytes 3538948
  54.9 3.9 %copy-start.18 = (bf16[4608,128]{1,0:T(8,128)(2,1)S(1)}, bf16[4608,128]{1,0:T(8,128)(2,1)}, u32[]{:S(2)}) copy-start(bf16[4608,128]{1,0:T(8,128)(2,1)} %param.16) | copy-start | bytes 3538948
  70.2 3.2 %copy-start.5 = (f32[256,64]{0,1:T(8,128)}, f32[256,64]{0,1:T(8,128)S(1)}, u32[]{:S(2)}) copy-start(f32[256,64]{0,1:T(8,128)S(1)} %get-tuple-element.57) | copy-start | bytes 196612
  70.2 3.2 %copy-start.7 = (f32[256,64]{0,1:T(8,128)}, f32[256,64]{0,1:T(8,128)S(1)}, u32[]{:S(2)}) copy-start(f32[256,64]{0,1:T(8,128)S(1)} %get-tuple-element.58) | copy-start | bytes 196612
  70.2 2.4 %copy-start.2 = (bf16[256,4608]{1,0:T(8,128)(2,1)S(1)}, bf16[256,4608]{1,0:T(8,128)(2,1)}, u32[]{:S(2)}) copy-start(bf16[256,4608]{1,0:T(8,128)(2,1)} %copy.66) | copy-start | bytes 7077892
  111.6 4.9 %copy-start.3 = (bf16[4096,2,128]{2,0,1:T(8,128)(2,1)S(1)}, bf16[4096,2,128]{2,0,1:T(8,128)(2,1)}, u32[]{:S(2)}) copy-start(bf16[4096,2,128]{2,0,1:T(8,128)(2,1)} %copy.47) | copy-start | bytes 6291460 | tf_op jit(solution)/shard_map/cond
  121.8 42.9 %all-to-all-start.1 = ((bf16[16,16,4608]{2,1,0:T(8,128)(2,1)}), bf16[16,16,4608]{2,1,0:T(8,128)(2,1)}, u32[]{:S(2)}, u32[]{:S(2)}) async-start(bf16[16,16,4608]{2,1,0:T(8,128)(2,1)} %bitcast.107), calls=%async_computation.1 | async-start | bytes 4718592 | tf_op jit(solution)/shard_map/all_to_all | solution.py:46
  131.1 35.8 %copy-start.4 = (bf16[16,4608]{1,0:T(8,128)(2,1)S(1)}, bf16[16,4608]{1,0:T(8,128)(2,1)}, u32[]{:S(2)}) copy-start(bf16[16,4608]{1,0:T(8,128)(2,1)} %copy.71) | copy-start | bytes 442372
  131.1 35.8 %copy-start.9 = (f32[4608]{0:T(1024)S(1)}, f32[4608]{0:T(1024)}, u32[]{:S(2)}) copy-start(f32[4608]{0:T(1024)} %param.19) | copy-start | bytes 55300
  168.7 38.1 %all-to-all-start.2 = ((bf16[16,16,4608]{2,1,0:T(8,128)(2,1)}), bf16[16,16,4608]{2,1,0:T(8,128)(2,1)}, u32[]{:S(2)}, u32[]{:S(2)}) async-start(bf16[16,16,4608]{2,1,0:T(8,128)(2,1)} %broadcast_in_dim.35), calls=%async_computation.2 | async-start | bytes 4718592 | tf_op jit(solution)/shard_map/all_to_all | solution.py:30
  173.3 4.4 %copy-start.16 = (s32[256]{0:T(256)S(1)}, s32[256]{0:T(256)}, u32[]{:S(2)}) copy-start(s32[256]{0:T(256)} %iota_add_fusion.1) | copy-start | bytes 3076
  177.7 31.3 %copy-start.11 = (f32[4608]{0:T(1024)S(1)}, f32[4608]{0:T(1024)}, u32[]{:S(2)}) copy-start(f32[4608]{0:T(1024)} %param.20) | copy-start | bytes 55300
  209.1 3.2 %copy-start.19 = (bf16[4608,128]{1,0:T(8,128)(2,1)S(1)}, bf16[4608,128]{1,0:T(8,128)(2,1)}, u32[]{:S(2)}) copy-start(bf16[4608,128]{1,0:T(8,128)(2,1)} %param.22) | copy-start | bytes 3538948
  212.2 2.8 %copy-start.13 = (f32[256]{0:T(256)S(1)}, f32[256]{0:T(256)}, u32[]{:S(2)}) copy-start(f32[256]{0:T(256)} %copy-done.12) | copy-start | bytes 3076
  212.2 2.8 %copy-start.15 = (f32[64]{0:T(128)S(1)}, f32[64]{0:T(128)}, u32[]{:S(2)}) copy-start(f32[64]{0:T(128)} %copy-done.14) | copy-start | bytes 772
  215.4 7.9 %copy-start.1 = (bf16[256,4608]{1,0:T(8,128)(2,1)S(1)}, bf16[256,4608]{1,0:T(8,128)(2,1)}, u32[]{:S(2)}) copy-start(bf16[256,4608]{1,0:T(8,128)(2,1)} %copy.68) | copy-start | bytes 7077892
  215.4 10.7 %collective-permute-start = (bf16[2,128,1,128]{1,3,2,0:T(8,128)(2,1)S(1)}, bf16[2,128,1,128]{1,3,2,0:T(8,128)(2,1)S(1)}, u32[]{:S(2)}, u32[]{:S(2)}) collective-permute-start(bf16[2,128,1,128]{1,3,2,0:T(8,128)(2,1)S(1)} %pad_maximum_fusion.2), channel_id=1, source_target_pairs={{0,16},{16,32},{32,48},{48,64},{64,80},{80,96},{96,112},{112,128},... | collective-permute-start | bytes 196616 | tf_op jit(solution)/shard_map/ppermute | solution.py:53
  223.3 0.8 copy-start.6
  223.3 0.9 copy-start.8
Sparse Core Ops, SparseCore 0:
  63.7 41.6 all-gather.1
where the time goes:
time: 235 us; the launch traced here: 234 us
  waiting for transfers between devices  129 us (55%)
  starting transfers between devices  24.4 us (10%)
  matrix products  24.1 us (10%)
  local copies, waits for them, and re-layouts  23.8 us (10%)
  other arithmetic  17.6 us (7%)
  between operations  15.1 us (6%)
    all_to_all x2, waiting for transfers between devices, copy_for_each(): lax.all_to_all(jnp.broadcast_to(array[None], (devices, *array.shape)), ax...  63.7 us
    all_to_all x1, waiting for transfers between devices, sent_and_summed(): lax.all_to_all(blocks, axis, split_axis=0, concat_axis=0, tiled=True)  33.7 us
    all_gather x1, waiting for transfers between devices, side_by_side(): result = lax.all_gather(both, axis, axis=dim, tiled=True)  31.8 us
    all_to_all x2, starting transfers between devices, copy_for_each(): lax.all_to_all(jnp.broadcast_to(array[None], (devices, *array.shape)), ax...  12.2 us
    dot_general x2, local copies, waits for them, and re-layouts, project_heads(): jnp.dot(normed, weight_query, preferred_element_type=jnp.float32)  8.74 us
    dot_general x2, matrix products, project_heads(): jnp.dot(normed, weight_value, preferred_element_type=jnp.float32)  7 us
    all_to_all x1, starting transfers between devices, sent_and_summed(): lax.all_to_all(blocks, axis, split_axis=0, concat_axis=0, tiled=True)  6.57 us
    dot_general x2, matrix products, project_heads(): jnp.dot(normed, weight_key, preferred_element_type=jnp.float32)  6.5 us
  transfers between devices with their start and end apart: 5, of which 4 were waited for; matrix products, arithmetic and copies ran while one was open for 9% of the time, Pallas kernels for 0%

commit v1 on v0

v1 whole, which is shorter than its diff:
```python
import functools
import math

import jax
import jax.numpy as jnp
from jax import lax
from jax.experimental import pallas as pl
from jax.experimental.pallas import tpu as pltpu
from jax.sharding import PartitionSpec as P

F32 = jnp.float32
BF16 = jnp.bfloat16
MESH = pl.DeviceIdType.MESH

D = 4608
ROWS = 256
SIDE = 4
SHARE = 16
COLS = 288
WIDE = 384
HALF = D // 2
QUARTER = D // 4
HEAD = 128
WINDOW = 128
NORM_EPS = 1e-06
SOFT_CAP = 50.0
SCORE_SCALE = float(D // 32) ** (-0.5) / SOFT_CAP
EXP_SCALE = SOFT_CAP * math.log2(math.e)


def mod(a, n):
    return lax.rem(a + n, n)


class Copies:
    def __init__(self, send_sems, recv_sems):
        self.send_sems, self.recv_sems = send_sems, recv_sems
        self.started = []

    def start(self, src, dst, device, when=None):
        k = len(self.started)
        copy = pltpu.make_async_remote_copy(
            src_ref=src,
            dst_ref=dst,
            send_sem=self.send_sems.at[k],
            recv_sem=self.recv_sems.at[k],
            device_id=device,
            device_id_type=MESH,
        )
        self.started.append((copy, when))
        if when is None:
            copy.start()
        else:
            pl.when(when)(copy.start)
        return copy

    def finish(self):
        for copy, when in self.started:
            if when is None:
                copy.wait_send()
            else:
                pl.when(when)(copy.wait_send)


def part_of(d):
    return 0 if d == 1 else 1


def gather_square(copies, piece, x, y, between):
    def place(h, first, second):
        dy, dx = (second, first) if h == 0 else (first, second)
        return mod(y + dy, SIDE), mod(x + dx, SIDE)

    def send(h, axis, d, first, second, part):
        by, bx = place(h, first, second)
        ty, tx = place(h, *((d, 0) if axis == 1 else (0, d)))
        ref = piece(by, bx, h, part)
        return copies.start(ref, ref, {"tp": ty * SIDE + tx})

    both = [(h, d) for h in (0, 1) for d in (1, -1)]
    near, far, side, last = {}, {}, {}, {}
    for h, d in both:
        near[h, d] = send(h, 1, d, 0, 0, None)
    for h, d in both:
        side[h, d, 0] = send(h, 2, d, 0, 0, None)
    between(0)
    for h, d in both:
        near[h, d].wait_recv()
        far[h, d] = send(h, 1, d, -d, 0, part_of(d))
        for e in (1, -1):
            side[h, e, -d] = send(h, 2, e, -d, 0, None)
    for h, d in both:
        side[h, d, 0].wait_recv()
        last[h, d, 0] = send(h, 2, d, 0, -d, part_of(d))
    between(1)
    for h in (0, 1):
        for d in (1, -1):
            far[h, d].wait_recv()
        for e in (1, -1):
            side[h, e, 2] = send(h, 2, e, 2, 0, None)
    for o in (1, -1):
        for h, d in both:
            side[h, d, o].wait_recv()
            last[h, d, o] = send(h, 2, d, o, -d, part_of(d))
    between(2)
    for h, d in both:
        side[h, d, 2].wait_recv()
        last[h, d, 2] = send(h, 2, d, 2, -d, part_of(d))
    for o in (0, 1, -1, 2):
        for h, d in both:
            last[h, d, o].wait_recv()
    between(3)


def sum_square(copies, terms, two, one, held, two_b, one_b, x, y):
    def place(h, along, across):
        dy, dx = (along, across) if h == 0 else (across, along)
        return mod(y + dy, SIDE), mod(x + dx, SIDE)

    def device(h, axis, d):
        ty, tx = place(h, *((d, 0) if axis == 1 else (0, d)))
        return {"tp": ty * SIDE + tx}

    def term(h, along, across, part=None):
        ty, tx = place(h, along, across)
        if part is None:
            return terms.at[ty, tx, :, pl.ds(HALF * h, HALF)]
        return terms.at[ty, tx, :, pl.ds(HALF * h + QUARTER * part, QUARTER)]

    def cut(ref, part):
        return ref.at[:, pl.ds(QUARTER * part, QUARTER)]

    def add(into, other):
        into[...] = (into[...].astype(F32) + other[...].astype(F32)).astype(BF16)

    both = [(h, d) for h in (0, 1) for d in (1, -1)]
    a, b, c = {}, {}, {}

    def send_far(e):
        for h, d in both:
            p = part_of(d)
            a[h, e, d] = copies.start(term(h, 2, e, p), two.at[h, e, p], device(h, 1, d))

    def send_raw(e):
        for h, d in both:
            p = part_of(d)
            b[h, e, d] = copies.start(
                term(h, d, e, 1 - p), cut(one.at[h, e, p], 1 - p), device(h, 1, d)
            )

    def send_summed(e):
        for h, d in both:
            p = part_of(d)
            a[h, e, d].wait_recv()
            mine = term(h, d, e, p)
            add(mine, two.at[h, e, p])
            c[h, e, d] = copies.start(mine, cut(one.at[h, e, p], p), device(h, 1, d))

    def total(e):
        for h in (0, 1):
            for d in (1, -1):
                b[h, e, d].wait_recv()
                c[h, e, d].wait_recv()
            held[h, e] = (
                term(h, 0, e)[...].astype(F32)
                + one[h, e, 0].astype(F32)
                + one[h, e, 1].astype(F32)
            ).astype(BF16)

    a2, b2, c2 = {}, {}, {}
    spot = {1: 1, -1: 3}

    def raw_b(d):
        p = part_of(d)
        for h in (0, 1):
            b2[h, d] = copies.start(
                cut(held.at[h, spot[d]], 1 - p), cut(one_b.at[h, p], 1 - p), device(h, 2, d)
            )

    send_far(2)
    send_far(1)
    send_far(3)
    send_raw(2)
    send_summed(2)
    send_far(0)
    send_raw(1)
    send_summed(1)
    send_raw(3)
    send_summed(3)
    total(2)
    for h, d in both:
        p = part_of(d)
        a2[h, d] = copies.start(cut(held.at[h, 2], p), two_b.at[h, p], device(h, 2, d))
    send_raw(0)
    send_summed(0)
    total(1)
    raw_b(1)
    total(3)
    raw_b(-1)
    for h, d in both:
        p = part_of(d)
        a2[h, d].wait_recv()
        mine = cut(held.at[h, spot[d]], p)
        add(mine, two_b.at[h, p])
        c2[h, d] = copies.start(mine, cut(one_b.at[h, p], p), device(h, 2, d))
    total(0)
    for h, d in both:
        b2[h, d].wait_recv()
        c2[h, d].wait_recv()
    return jnp.concatenate(
        [
            held[h, 0].astype(F32) + one_b[h, 0].astype(F32) + one_b[h, 1].astype(F32)
            for h in (0, 1)
        ],
        axis=1,
    )


def turned(u, cosines, sines):
    return u * cosines + pltpu.roll(u, HEAD // 2, 1) * sines


def weights_of(queries, keys):
    s = lax.dot_general(queries, keys, (((1,), (1,)), ((), ())), preferred_element_type=F32)
    return jnp.exp2(jnp.tanh(s * SCORE_SCALE) * EXP_SCALE)


def kernel(
    nz, nc,
    tok, gain1, post, gain2, wq, wk, wv, wo, lq, lk, lv,
    hidden_out, heads_out,
    T, W1, W2, WO, acc, ssq, cosines, sines, Q, KV, num, den, att,
    terms, two, one, held, two_b, one_b, own, H, HS, LKV,
    send_sems, recv_sems, load_sems,
):
    t = lax.axis_index("tp")
    s = lax.axis_index("seq")
    y, x = lax.div(t, SIDE), lax.rem(t, SIDE)
    z, c = lax.div(s, nc), lax.rem(s, nc)
    ns = nz * nc

    barrier = pltpu.get_barrier_semaphore()
    peers = [
        {"tp": y * SIDE + mod(x + 1, SIDE)},
        {"tp": y * SIDE + mod(x - 1, SIDE)},
        {"tp": mod(y + 1, SIDE) * SIDE + x},
        {"tp": mod(y - 1, SIDE) * SIDE + x},
    ]
    if ns > 1:
        peers += [
            {"seq": mod(z + 1, nz) * nc + c},
            {"seq": mod(z - 1, nz) * nc + c},
            {"seq": z * nc + 1 - c},
            {"seq": mod(s - 1 + 2 * c, ns)},
        ]
    for peer in peers:
        pl.semaphore_signal(barrier, inc=1, device_id=peer, device_id_type=MESH)

    loads = []

    def load(src, dst):
        copy = pltpu.make_async_copy(src, dst, load_sems.at[len(loads)])
        copy.start()
        loads.append(copy)

    for w, at, width in ((wq, 0, 256), (wk, 256, 128), (wv, 384, 128)):
        load(w.at[:, pl.ds(0, 256), :], W1.at[:, pl.ds(0, 256), pl.ds(at, width)])
        for k in range(4):
            load(w.at[:, pl.ds(256, 32), :], W1.at[:, pl.ds(256 + 32 * k, 32), pl.ds(at, width)])
    first_loads = len(loads)
    load(wo, WO)
    load(lk, W2.at[:, pl.ds(256, 128)])
    load(lv, W2.at[:, pl.ds(384, 128)])
    load(lq, W2.at[:, pl.ds(0, 256)])

    T[y, x, 0, 0:ROWS, :] = tok[:, 0:128]
    T[y, x, 1, 0:ROWS, :] = tok[:, 128:256]
    for half in (0, 1):
        T[y, x, half, ROWS:COLS, :] = jnp.concatenate(
            [tok[32 * (4 * half + k) : 32 * (4 * half + k + 1), 256:288] for k in range(4)], axis=1
        )
    pl.semaphore_wait(barrier, len(peers))

    copies = Copies(send_sems, recv_sems)

    row = lax.broadcasted_iota(jnp.int32, (ROWS, HEAD), 0)
    lane = lax.broadcasted_iota(jnp.int32, (ROWS, HEAD), 1)
    tail_mask = lax.rem(lax.div(row, 32), 4) == lax.div(lane, 32)

    def take(by, bx):
        k = by * SIDE + bx
        tails = [T[by, bx, half, ROWS:COLS, :].astype(F32) for half in (0, 1)]
        parts = [
            T[by, bx, 0, 0:ROWS, :].astype(F32),
            T[by, bx, 1, 0:ROWS, :].astype(F32),
            jnp.where(tail_mask, jnp.concatenate([tails[0]] * 4 + [tails[1]] * 4, axis=0), 0.0),
        ]
        ssq[...] += sum(u * u for u in parts)
        gain = gain1[pl.ds(k, 1), :]
        scaled = jnp.concatenate(
            [(u * gain[:, HEAD * i : HEAD * (i + 1)]).astype(BF16) for i, u in enumerate(parts)],
            axis=1,
        )
        acc[...] += jnp.dot(scaled, W1[k], preferred_element_type=F32)

    def take_offset(dy, dx):
        take(mod(y + dy, SIDE), mod(x + dx, SIDE))

    def over(count, body):
        def step(i, carry):
            body(i)
            return carry

        lax.fori_loop(0, count, step, 0)

    def between_first(stage):
        if stage == 0:
            half_lane = jnp.where(lane < HEAD // 2, lane, lane - HEAD // 2)
            frequency = jnp.exp(half_lane.astype(F32) * (-math.log(10000.0) / (HEAD // 2)))
            angle = (row + s * ROWS).astype(F32) * frequency
            cosines[...] = jnp.cos(angle)
            sine = jnp.sin(angle)
            sines[...] = jnp.where(lane < HEAD // 2, -sine, sine)
            acc[...] = jnp.zeros_like(acc)
            ssq[...] = jnp.zeros_like(ssq)
            num[...] = jnp.zeros_like(num)
            den[...] = jnp.zeros_like(den)
        elif stage == 1:
            for copy in loads[:first_loads]:
                copy.wait()
            take_offset(0, 0)

            def near(i):
                step, alongside = 1 + 2 * lax.rem(i, 2), lax.div(i, 2)
                take_offset(step * alongside, step * (1 - alongside))

            over(4, near)
        elif stage == 2:
            over(4, lambda i: take_offset(1 + 2 * lax.rem(i, 2), 1 + 2 * lax.div(i, 2)))
        elif stage == 3:
            over(4, lambda i: take_offset(2, i))
            over(3, lambda i: take_offset(i + lax.div(i, 2), 2))

    def block(by, bx, h, part):
        if part is None:
            return T.at[by, bx, h]
        return T.at[by, bx, h, pl.ds(144 * part, 144), :]

    gather_square(copies, block, x, y, between_first)

    def scale_of(squares):
        return lax.rsqrt(jnp.sum(squares, axis=1, keepdims=True) * (1.0 / D) + NORM_EPS)

    factor = scale_of(ssq[...])
    ring = {}

    def send_along(dirn, hop, kv):
        zb = mod(z - dirn * (hop - 1), nz)
        ref = KV.at[zb, c, kv]
        ring[dirn, hop, kv] = copies.start(ref, ref, {"seq": mod(z + dirn, nz) * nc + c})

    def send_across(dirn, hop, kv):
        ref = KV.at[mod(z - dirn * hop, nz), c, kv]
        ring["across", dirn, hop, kv] = copies.start(ref, ref, {"seq": z * nc + 1 - c})

    def allowed(dirn, hop, kv):
        return hop <= 3 or (hop == 4 and (dirn == 1) == (kv == 0))

    KV[z, c, 0] = turned(acc[:, 256:384] * factor, cosines[...], sines[...]).astype(BF16)
    if ns > 1:
        for dirn in (1, -1):
            send_along(dirn, 1, 0)
    KV[z, c, 1] = (acc[:, 384:512] * factor).astype(BF16)
    if ns > 1:
        for dirn in (1, -1):
            send_along(dirn, 1, 1)
        for kv in (0, 1):
            send_across(1, 0, kv)
    for h in (0, 1):
        Q[ROWS * h : ROWS * (h + 1), :] = turned(
            acc[:, HEAD * h : HEAD * (h + 1)] * factor, cosines[...], sines[...]
        ).astype(BF16)

    def attend(zb, cb, causal):
        for i in range(4):
            at = pl.ds(128 * i, 128)
            w = weights_of(Q[at, :], KV[zb, cb, 0])
            if causal:
                r = lax.broadcasted_iota(jnp.int32, w.shape, 0) + 128 * (i % 2)
                w = jnp.where(lax.broadcasted_iota(jnp.int32, w.shape, 1) <= r, w, 0.0)
            den[at, :] += w[:, 0:128] + w[:, 128:256]
            num[at, :] += jnp.dot(w.astype(BF16), KV[zb, cb, 1], preferred_element_type=F32)

    def attend_if(zb, cb):
        @pl.when(zb * nc + cb < s)
        def _():
            attend(zb, cb, False)

    attend(z, c, True)

    own[...] = jnp.zeros_like(own)
    tail_lane = lax.broadcasted_iota(jnp.int32, (SHARE, HEAD), 1)
    for k in range(16):
        by, bx = divmod(k, SIDE)
        rows = pl.ds(pl.multiple_of(t * SHARE, SHARE), SHARE)
        tail_rows = pl.ds(pl.multiple_of(ROWS + SHARE * lax.rem(t, 2), SHARE), SHARE)
        tail = T[by, bx, lax.div(t, 8), tail_rows, :].astype(F32)
        tail = pltpu.roll(tail, lax.rem(HEAD - 32 * lax.rem(lax.div(t, 2), 4), HEAD), 1)
        joined = jnp.concatenate(
            [
                T[by, bx, 0, rows, :].astype(F32),
                T[by, bx, 1, rows, :].astype(F32),
                jnp.where(tail_lane < 32, tail, 0.0),
            ],
            axis=1,
        )
        start = 128 * (2 * k + k // 4)
        if k % 4:
            joined = pltpu.roll(joined, 32 * (k % 4), 1)
        own[:, start : start + WIDE] += joined

    if ns > 1:
        def across(dirn, hop):
            for kv in (0, 1):
                if allowed(dirn, hop, kv):
                    ring["across", dirn, hop, kv].wait_recv()

        for hop in (1, 2, 3, 4):
            for kv in (0, 1):
                for dirn in (1, -1):
                    if allowed(dirn, hop, kv):
                        ring[dirn, hop, kv].wait_recv()
                        if allowed(dirn, hop + 1, kv):
                            send_along(dirn, hop + 1, kv)
                        send_across(dirn, hop, kv)
            if hop < 4:
                over(2, lambda i, hop=hop: attend_if(mod(z - hop + 2 * hop * i, nz), c))
            else:
                attend_if(mod(z - 4, nz), c)
            if hop == 1:
                across(1, 0)
                attend_if(z, 1 - c)
            else:
                across(1, hop - 1)
                across(-1, hop - 1)
                over(2, lambda i, hop=hop: attend_if(mod(z - (hop - 1) + 2 * (hop - 1) * i, nz), 1 - c))
        across(1, 4)
        across(-1, 4)
        attend_if(mod(z - 4, nz), 1 - c)

    for h in (0, 1):
        at = pl.ds(ROWS * h, ROWS)
        att[:, HEAD * h : HEAD * (h + 1)] = (
            num[at, :] / jnp.sum(den[at, :], axis=1, keepdims=True)
        ).astype(BF16)

    for copy in loads[first_loads:]:
        copy.wait()
    for n in range(D // 512):
        product = jnp.dot(att[...], WO[:, 512 * n : 512 * (n + 1)], preferred_element_type=F32)
        terms[:, :, :, 512 * n : 512 * (n + 1)] = product.astype(BF16).reshape(SIDE, SIDE, SHARE, 512)
    summed = sum_square(copies, terms, two, one, held, two_b, one_b, x, y)
    level = lax.rsqrt(jnp.sum(summed * summed, axis=1, keepdims=True) * (1.0 / D) + NORM_EPS)
    H[y, x] = (own[...] + summed * level * post[...]).astype(BF16)

    ssq[...] = jnp.zeros_like(ssq)

    def scaled_rows(by, bx):
        k = by * SIDE + bx
        rows = H[by, bx].astype(F32)
        HS[k] = (rows * gain2[...]).astype(BF16)
        squares = rows * rows
        ssq[pl.ds(pl.multiple_of(k * SHARE, SHARE), SHARE), :] = sum(
            squares[:, HEAD * i : HEAD * (i + 1)] for i in range(D // HEAD)
        )

    def between_second(stage):
        def at(dy, dx):
            scaled_rows(mod(y + dy, SIDE), mod(x + dx, SIDE))

        if stage == 1:
            at(0, 0)

            def near(i):
                step, alongside = 1 + 2 * lax.rem(i, 2), lax.div(i, 2)
                at(step * alongside, step * (1 - alongside))

            over(4, near)
        elif stage == 2:
            over(4, lambda i: at(1 + 2 * lax.rem(i, 2), 1 + 2 * lax.div(i, 2)))
        elif stage == 3:
            over(4, lambda i: at(2, i))
            over(3, lambda i: at(i + lax.div(i, 2), 2))

    def hidden_block(by, bx, h, part):
        if part is None:
            return H.at[by, bx, :, pl.ds(HALF * h, HALF)]
        return H.at[by, bx, :, pl.ds(HALF * h + QUARTER * part, QUARTER)]

    gather_square(copies, hidden_block, x, y, between_second)

    factor = scale_of(ssq[...])
    rows = HS[...].reshape(ROWS, D)
    pair = jnp.dot(rows, W2[:, 256:512], preferred_element_type=F32) * factor
    LKV[0, WINDOW : WINDOW + ROWS, :] = turned(pair[:, 0:128], cosines[...], sines[...]).astype(BF16)
    LKV[1, WINDOW : WINDOW + ROWS, :] = pair[:, 128:256].astype(BF16)
    handed = []
    if ns > 1:
        for kv in (0, 1):
            handed.append(
                copies.start(
                    LKV.at[kv, pl.ds(ROWS, WINDOW), :],
                    LKV.at[kv, pl.ds(0, WINDOW), :],
                    {"seq": mod(s + 1, ns)},
                    when=s < ns - 1,
                )
            )

    @pl.when(s == 0)
    def _():
        LKV[:, 0:WINDOW, :] = jnp.zeros((2, WINDOW, HEAD), BF16)

    local_q = jnp.dot(rows, W2[:, 0:256], preferred_element_type=F32) * factor
    for h in (0, 1):
        Q[ROWS * h : ROWS * (h + 1), :] = turned(
            local_q[:, HEAD * h : HEAD * (h + 1)], cosines[...], sines[...]
        ).astype(BF16)

    base = pl.multiple_of(128 * (2 * t + lax.div(t, 4)), 128)
    window = H[:, :, :, pl.ds(base, WIDE)].reshape(ROWS, WIDE).astype(F32)
    window = pltpu.roll(window, lax.rem(WIDE - 32 * lax.rem(t, 4), WIDE), 1)
    hidden_out[...] = window[:, 0:COLS].astype(BF16)

    def attend_window(b):
        for h in (0, 1):
            at = pl.ds(ROWS * h + WINDOW * b, WINDOW)
            span = pl.ds(WINDOW * b, 2 * WINDOW)
            w = weights_of(Q[at, :], LKV[0, span, :])
            r = lax.broadcasted_iota(jnp.int32, w.shape, 0)
            k = lax.broadcasted_iota(jnp.int32, w.shape, 1)
            mask = (k > r) & (k <= r + WINDOW)
            if b == 0:
                mask = mask & ((k >= WINDOW) | (s > 0))
            w = jnp.where(mask, w, 0.0)
            below = jnp.sum(w, axis=1, keepdims=True)
            above = jnp.dot(w.astype(BF16), LKV[1, span, :], preferred_element_type=F32)
            heads_out[WINDOW * b : WINDOW * (b + 1), HEAD * h : HEAD * (h + 1)] = (
                above / below
            ).astype(BF16)

    attend_window(1)
    for copy in handed:
        pl.when(s > 0)(copy.wait_recv)
    attend_window(0)
    copies.finish()


COPIES = 176


def local(
    nz, nc,
    tokens, attention_gain, query_weight, key_weight, value_weight, output_weight,
    post_gain, local_gain, local_query_weight, local_key_weight, local_value_weight,
):
    blocks = attention_gain.reshape(16, COLS)
    gain1 = jnp.concatenate([blocks[:, :256]] + [blocks[:, 256:]] * 4, axis=1)
    vmem = pl.BlockSpec(memory_space=pltpu.VMEM)
    hbm = pl.BlockSpec(memory_space=pl.ANY)
    ns = nz * nc
    return pl.pallas_call(
        functools.partial(kernel, nz, nc),
        out_shape=(
            jax.ShapeDtypeStruct((ROWS, COLS), BF16),
            jax.ShapeDtypeStruct((ROWS, 256), BF16),
        ),
        in_specs=[vmem] * 4 + [hbm] * 7,
        out_specs=(vmem, vmem),
        scratch_shapes=[
            pltpu.VMEM((SIDE, SIDE, 2, COLS, 128), BF16),
            pltpu.VMEM((16, WIDE, 512), BF16),
            pltpu.VMEM((D, 512), BF16),
            pltpu.VMEM((256, D), BF16),
            pltpu.VMEM((ROWS, 512), F32),
            pltpu.VMEM((ROWS, HEAD), F32),
            pltpu.VMEM((ROWS, HEAD), F32),
            pltpu.VMEM((ROWS, HEAD), F32),
            pltpu.VMEM((2 * ROWS, HEAD), BF16),
            pltpu.VMEM((nz, nc, 2, ROWS, HEAD), BF16),
            pltpu.VMEM((2 * ROWS, HEAD), F32),
            pltpu.VMEM((2 * ROWS, HEAD), F32),
            pltpu.VMEM((ROWS, 256), BF16),
            pltpu.VMEM((SIDE, SIDE, SHARE, D), BF16),
            pltpu.VMEM((2, 4, 2, SHARE, QUARTER), BF16),
            pltpu.VMEM((2, 4, 2, SHARE, HALF), BF16),
            pltpu.VMEM((2, 4, SHARE, HALF), BF16),
            pltpu.VMEM((2, 2, SHARE, QUARTER), BF16),
            pltpu.VMEM((2, 2, SHARE, HALF), BF16),
            pltpu.VMEM((SHARE, D), F32),
            pltpu.VMEM((SIDE, SIDE, SHARE, D), BF16),
            pltpu.VMEM((16, SHARE, D), BF16),
            pltpu.VMEM((2, WINDOW + ROWS, HEAD), BF16),
            pltpu.SemaphoreType.DMA((COPIES,)),
            pltpu.SemaphoreType.DMA((COPIES,)),
            pltpu.SemaphoreType.DMA((24,)),
        ],
        compiler_params=pltpu.CompilerParams(
            collective_id=0, has_side_effects=True, vmem_limit_bytes=56 * 1024 * 1024
        ),
    )(
        tokens, gain1, post_gain.reshape(1, D), local_gain.reshape(1, D),
        query_weight.reshape(16, COLS, -1), key_weight.reshape(16, COLS, -1),
        value_weight.reshape(16, COLS, -1), output_weight,
        local_query_weight, local_key_weight, local_value_weight,
    )


def solution(mesh):
    in_specs = (
        P("seq", "tp"),
        P(),
        P(None, "tp"),
        P(None, "tp"),
        P(None, "tp"),
        P("tp", None),
        P(),
        P(),
        P(None, "tp"),
        P(None, "tp"),
        P(None, "tp"),
    )
    out_specs = (P("seq", "tp"), P("seq", "tp"))
    ns = mesh.shape["seq"]
    nc = 2 if ns > 1 else 1
    return jax.shard_map(
        functools.partial(local, ns // nc, nc),
        mesh=mesh,
        in_specs=in_specs,
        out_specs=out_specs,
        check_vma=False,
    )
```

time: 235 us -> 98.5 us (0.42)
  waiting for transfers between devices: 129 us -> 0 us
  Pallas kernels: 0 us -> 88.4 us
  starting transfers between devices: 24.4 us -> 0 us
  matrix products: 24.1 us -> 0 us
  other arithmetic: 17.6 us -> 0.69 us
  local copies, waits for them, and re-layouts: 23.8 us -> 8.48 us
  between operations: 15.1 us -> 0.64 us
    all_to_all x3 -> x0, waiting for transfers between devices: 97.3 us -> none  [the longest x2 63.7 us: copy_for_each(): lax.all_to_all(jnp.broadcast_to(array[None], (devices, *array.shape)), ax...]
    pallas_call x0 -> x1, Pallas kernels: none -> 88.4 us  [local(): pl.pallas_call(functools.partial(kernel, nz, nc), out_shape=(jax.ShapeDty...]
    all_gather x1 -> x0, waiting for transfers between devices: 31.8 us -> none  [side_by_side(): result = lax.all_gather(both, axis, axis=dim, tiled=True)]
    dot_general x11 -> x0, matrix products: 24.1 us -> none  [the longest x2 7 us: project_heads(): jnp.dot(normed, weight_value, preferred_element_type=jnp.float32)]
    all_to_all x3 -> x0, starting transfers between devices: 18.8 us -> none  [the longest x2 12.2 us: copy_for_each(): lax.all_to_all(jnp.broadcast_to(array[None], (devices, *array.shape)), ax...]
    dot_general x2 -> x0, local copies, waits for them, and re-layouts: 8.74 us -> none  [project_heads(): jnp.dot(normed, weight_query, preferred_element_type=jnp.float32)]
    reduce_sum x4 -> x0, other arithmetic: 6.75 us -> none  [the longest x3 4.74 us: rms_scaled(): jnp.mean(widened * widened, axis=-1, keepdims=True) + NORM_EPS]
    convert_element_type x5 -> x0, other arithmetic: 5.64 us -> none  [the longest x1 2.34 us: local(): local_normed = rms_scaled(whole_hidden, local_gain).astype(jnp.bfloat16)]
  transfers between devices with their start and end apart: 5 -> 0, of which waited for: 4 -> 0; matrix products, arithmetic and copies ran while one was open for 9% -> 0% of each run, Pallas kernels for 0% -> 0%
where the time goes in v1:
time: 98.5 us; the launch traced here: 98.2 us
  Pallas kernels  88.4 us (90%)
  local copies, waits for them, and re-layouts  8.48 us (9%)
    pallas_call x1, Pallas kernels, local(): pl.pallas_call(functools.partial(kernel, nz, nc), out_shape=(jax.ShapeDty...  88.4 us
    unnamed x2, local copies, waits for them, and re-layouts  3.29 us

profile of v1, /device:TPU:1, one launch (start us, length us, event | category | flops | bytes accessed | tf_op | source)
XLA Modules:
  0.0 98.2 jit_solution(12426389532481358556)
XLA Ops:
  0.6 1.3 %reshape.23.post = f32[1,4608]{1,0:T(1,128)} reshape(f32[4608]{0:T(1024)} %param.17) | data formatting | bytes 36864 | tf_op jit(solution)/shard_map/reshape | solution.py:611
  2.0 1.3 %reshape.24.gain2 = f32[1,4608]{1,0:T(1,128)} reshape(f32[4608]{0:T(1024)} %param.18) | data formatting | bytes 36864 | tf_op jit(solution)/shard_map/reshape | solution.py:611
  3.3 0.8 reshape.22
  4.1 0.7 pad_maximum_fusion.gain1
  4.8 1.7 %copy.13.tok = bf16[256,288]{1,0:T(8,128)(2,1)} copy(bf16[256,288]{0,1:T(8,128)(2,1)} %param.11) | data formatting | bytes 294912 | tf_op args[0]
  6.5 88.4 %shard_map.122 = (bf16[256,288]{1,0:T(8,128)(2,1)}, bf16[256,256]{1,0:T(8,128)(2,1)}) custom-call(bf16[256,288]{1,0:T(8,128)(2,1)} %copy.13.tok, f32[16,384]{1,0:T(8,128)} %pad_maximum_fusion.gain1, f32[1,4608]{1,0:T(1,128)} %reshape.23.post, f32[1,4608]{1,0:T(1,128)} %reshape.24.gain2, bf16[16,288,256]{2,1,0:T(8,128)(2,1)} %bitcast.3, ...), custom_call_target="tpu_custom_call" | custom-call | tf_op jit(solution)/shard_map/pallas_call | solution.py:571
  94.9 1.7 %copy.14 = bf16[256,288]{0,1:T(8,128)(2,1)} copy(bf16[256,288]{1,0:T(8,128)(2,1)} %get-tuple-element.2) | data formatting | bytes 294912 | tf_op jit(solution)/shard_map/pallas_call | solution.py:571
  96.6 1.6 %copy.16 = bf16[256,256]{1,0:T(8,128)(2,1)} copy(bf16[256,256]{1,0:T(8,128)(2,1)} %get-tuple-element.7) | data formatting | bytes 262144
  (1 shorter events, 0.0 us)
